TPU v7x, 256 devices: a whole 4x4x8 slice. The times are simulated.
256 devices in a mesh: dp: 16 (over x, y_hi, core), pencil: 16 (over z, y_lo).
Axes of the slice: x: 4, y: 4 (y_hi: 2, y_lo: 2; y = y_hi * 2 + y_lo), z: 8, core: 2. Of those that a mesh axis runs over, the one named last changes fastest.
Arguments:
- field: bfloat16 [16, 64, 64, 64, 128], P('dp', 'pencil'), may hold values from -6 to 6
- cotangent: bfloat16 [16, 64, 64, 64, 128], P('dp', 'pencil'), may hold values from -6 to 6
- w_spec: bfloat16 [16, 16, 16, 64, 128], P('dp', 'pencil'), may hold values from -6 to 6
- w_local: bfloat16 [64, 64], replicated, may hold values from -0.75 to 0.75
Outputs:
- grad_field: bfloat16 [16, 64, 64, 64, 128], P('dp', 'pencil')
- grad_w: float32 [16, 16, 16, 64, 128], P('dp', 'pencil')
All inputs are finite; a program needn't handle non-finite values.
Results may differ from a plain program's by a relative error of at most 0.02.
Values may be sent and summed in bfloat16 or wider, within the bound.
A program may use at most 128 MiB of HBM per device.

v0:
```python
import math
import jax
import jax.numpy as jnp
from jax import lax
from jax.sharding import PartitionSpec as P

NX = 64
NY = 64
NZ = 128
CH = 64
MX = 16
MY = 16
MZ = 16


def phase_pair(length, mode_count, signed):
    position = jnp.arange(length, dtype=jnp.int32)
    indices = jnp.arange(mode_count, dtype=jnp.int32)
    frequency = (
        jnp.where(indices < mode_count // 2, indices, indices - mode_count) if signed else indices
    )
    product = jnp.mod(position[:, None] * frequency[None, :], length).astype(jnp.float32)
    angles = product * (2.0 * math.pi / length)
    return (jnp.cos(angles), jnp.sin(angles))


def grid_tables():
    cos_x, sin_x = phase_pair(NX, MX, True)
    cos_y, sin_y = phase_pair(NY, MY, True)
    cos_z, sin_z = phase_pair(NZ, MZ, False)
    forward_z = jnp.concatenate([cos_z, -sin_z], 1).astype(jnp.bfloat16)
    weight_z = jnp.where(jnp.arange(MZ, dtype=jnp.int32) == 0, 1.0, 2.0).astype(jnp.float32) / (
        NX * NY * NZ
    )
    inverse_z = jnp.concatenate([cos_z * weight_z, -sin_z * weight_z], 1).T
    adjoint_z = jnp.concatenate([cos_z, -sin_z], 1).T
    spectrum_scale = jnp.concatenate([weight_z, weight_z])
    return (cos_x, sin_x, cos_y, sin_y, forward_z, inverse_z, adjoint_z, spectrum_scale)


def rotate_half(values):
    middle = values.shape[-1] // 2
    return jnp.concatenate([values[..., middle:], -values[..., :middle]], -1)


def along_y(values, cosines, sine_table, inverse):
    pattern = "xjck,yj->xyck" if inverse else "xyck,yj->xjck"
    factor = -1.0 if inverse else 1.0
    direct = jnp.einsum(pattern, values, cosines)
    turned = jnp.einsum(pattern, rotate_half(values), sine_table)
    return direct + factor * turned


def along_x(values, cosines, sine_table, inverse):
    pattern = "jbck,xj->xbck" if inverse else "xbck,xj->jbck"
    factor = -1.0 if inverse else 1.0
    direct = jnp.einsum(pattern, values, cosines)
    turned = jnp.einsum(pattern, rotate_half(values), sine_table)
    return direct + factor * turned


def z_forward(field_in, matrix):
    shape_in = field_in.shape
    product = jnp.dot(
        field_in.reshape(-1, shape_in[-1]), matrix, preferred_element_type=jnp.float32
    )
    return product.reshape(shape_in[:-1] + (matrix.shape[1],))


def z_back(values, matrix):
    shape_in = values.shape
    product = jnp.dot(values.reshape(-1, shape_in[-1]), matrix, preferred_element_type=jnp.float32)
    return product.reshape(shape_in[:-1] + (matrix.shape[1],))


def gelu_slope(pre):
    normal_cdf = 0.5 * (1.0 + lax.erf(pre * (1.0 / math.sqrt(2.0))))
    return normal_cdf + pre * jnp.exp(-0.5 * pre * pre) * (1.0 / math.sqrt(2.0 * math.pi))


def apply_modes(coeffs, weights):
    real_part = coeffs[..., :MZ]
    imag_part = coeffs[..., MZ:]
    from_real = jnp.einsum(
        "sabik,abkio->sabok", real_part, weights, preferred_element_type=jnp.float32
    )
    from_imag = jnp.einsum(
        "sabik,abkio->sabok", imag_part, weights, preferred_element_type=jnp.float32
    )
    out_real = from_real[:, :, :, :CH] - from_imag[:, :, :, CH:]
    out_imag = from_real[:, :, :, CH:] + from_imag[:, :, :, :CH]
    return jnp.concatenate([out_real, out_imag], -1)


def paired(g_modes):
    g_real = g_modes[..., :MZ]
    g_imag = g_modes[..., MZ:]
    return (jnp.concatenate([g_real, g_imag], -2), jnp.concatenate([g_imag, -g_real], -2))


def adjoint_modes(g_modes, weights):
    paired_one, paired_two = paired(g_modes)
    back_real = jnp.einsum(
        "abkio,sabok->sabik", weights, paired_one, preferred_element_type=jnp.float32
    )
    back_imag = jnp.einsum(
        "abkio,sabok->sabik", weights, paired_two, preferred_element_type=jnp.float32
    )
    return jnp.concatenate([back_real, back_imag], -1)


def mode_grads(u_modes, g_modes):
    paired_one, paired_two = paired(g_modes)
    from_real = jnp.einsum(
        "sabik,sabok->abkio", u_modes[..., :MZ], paired_one, preferred_element_type=jnp.float32
    )
    from_imag = jnp.einsum(
        "sabik,sabok->abkio", u_modes[..., MZ:], paired_two, preferred_element_type=jnp.float32
    )
    return from_real + from_imag


def to_modes(field_in, tables):
    cos_x, sin_x, cos_y, sin_y, forward_z = (tables[0], tables[1], tables[2], tables[3], tables[4])
    sectioned = along_y(z_forward(field_in, forward_z), cos_y, sin_y, False)
    arrived = lax.all_to_all(
        sectioned.astype(jnp.bfloat16), "pencil", split_axis=1, concat_axis=0, tiled=True
    ).astype(sectioned.dtype)
    return along_x(arrived, cos_x, sin_x, False)


def to_grid(coeffs, tables, matrix):
    cos_x, sin_x, cos_y, sin_y = (tables[0], tables[1], tables[2], tables[3])
    sectioned = along_x(coeffs, cos_x, sin_x, True)
    arrived = lax.all_to_all(
        sectioned.astype(jnp.bfloat16), "pencil", split_axis=0, concat_axis=1, tiled=True
    ).astype(sectioned.dtype)
    return z_back(along_y(arrived, cos_y, sin_y, True), matrix)


def to_owner(coeffs):
    return lax.all_to_all(coeffs[None], "dp", split_axis=1, concat_axis=0, tiled=True)


def from_owner(coeffs):
    return lax.all_to_all(
        coeffs.astype(jnp.bfloat16), "dp", split_axis=0, concat_axis=1, tiled=True
    ).astype(coeffs.dtype)[0]


def body(field, cotangent, w_spec, w_local):
    tables = grid_tables()
    inverse_z, adjoint_z, spectrum_scale = (tables[5], tables[6], tables[7])
    sample = field[0]
    target = cotangent[0]
    u_modes = to_modes(sample, tables).astype(jnp.bfloat16)
    u_sent = to_owner(u_modes)
    v_modes = from_owner(apply_modes(u_sent, w_spec))
    values = to_grid(v_modes, tables, inverse_z)
    bypass = jnp.einsum("xycz,co->xyoz", sample, w_local, preferred_element_type=jnp.float32)
    slope_in = (target.astype(jnp.float32) * gelu_slope(values + bypass)).astype(jnp.bfloat16)
    g_modes = (to_modes(slope_in, tables) * spectrum_scale).astype(jnp.bfloat16)
    g_sent = to_owner(g_modes)
    grad_w = mode_grads(u_sent, g_sent)
    back_modes = from_owner(adjoint_modes(g_sent, w_spec))
    spread = jnp.einsum("xyoz,co->xycz", slope_in, w_local, preferred_element_type=jnp.float32)
    grad_sample = (to_grid(back_modes, tables, adjoint_z) + spread).astype(jnp.bfloat16)
    return (grad_sample[None], grad_w)


def solution(mesh):
    placed = (
        P("dp", "pencil", None, None, None),
        P("dp", "pencil", None, None, None),
        P("dp", "pencil", None, None, None),
        P(),
    )
    return jax.shard_map(
        body,
        mesh=mesh,
        in_specs=placed,
        out_specs=(P("dp", "pencil", None, None, None), P("dp", "pencil", None, None, None)),
        check_vma=False,
    )
```

profile of v0, /device:TPU:1, one launch (start us, length us, event | category | flops | bytes accessed | tf_op | source)
XLA Modules:
  0.0 167.1 jit_solution(9578072925121026040)
XLA Ops:
  0.7 3.7 %convolution_bitcast_fusion = f32[16384,32]{0,1:T(8,128)S(1)} fusion(bf16[16384,128]{1,0:T(8,128)(2,1)} %bitcast.246, bf16[128,16]{0,1:T(8,128)(2,1)S(1)} %get-tuple-element.21, bf16[128,16]{0,1:T(8,128)(2,1)S(1)} %get-tuple-element.22), kind=kOutput, calls=%fused_computation | convolution fusion | flops 134234112 | bytes 6299648 | tf_op jit(solution)/shard_map/dot_general | solution.py:64
  4.4 3.0 %reshape.248 = f32[4,64,64,32]{2,1,0,3:T(8,128)} reshape(f32[16384,32]{0,1:T(8,128)S(1)} %convolution_bitcast_fusion) | data formatting | bytes 4194304 | tf_op jit(solution)/shard_map/reshape | solution.py:67
  7.5 3.0 %fusion.229 = (bf16[4,64,64,16]{2,1,3,0:T(8,128)(2,1)S(1)}, bf16[4,64,64,16]{2,1,3,0:T(8,128)(2,1)S(1)}) fusion(f32[4,64,64,32]{2,1,0,3:T(8,128)} %reshape.248), kind=kLoop, calls=%fused_computation.258 | loop fusion | flops 524288 | bytes 4194304 | tf_op jit(solution)/shard_map/slice | solution.py:43
  12.6 20.5 %all_to_all.108 = bf16[16,2,4096]{2,1,0:T(2,128)(2,1)S(1)} all-to-all(bf16[16,2,4096]{2,1,0:T(2,128)(2,1)S(1)} %reshape.276), channel_id=1, replica_groups=mesh['dp'=16,'pencil'=16] {'pencil'}, dimensions={0} | all-to-all | bytes 524288 | tf_op jit(solution)/shard_map/all_to_all | solution.py:126
  35.4 9.0 %all-to-all-start.1 = ((bf16[16,2,1024]{2,1,0:T(2,128)(2,1)}), bf16[16,2,1024]{2,1,0:T(2,128)(2,1)S(1)}, u32[]{:S(2)}, u32[]{:S(2)}) async-start(bf16[16,2,1024]{2,1,0:T(2,128)(2,1)} %reshape.278), calls=%async_computation.1 | async-start | bytes 131072 | tf_op jit(solution)/shard_map/all_to_all | solution.py:142
  44.4 7.4 %all-to-all-done.1 = bf16[16,2,1024]{2,1,0:T(2,128)(2,1)S(1)} async-done(((bf16[16,2,1024]{2,1,0:T(2,128)(2,1)}), bf16[16,2,1024]{2,1,0:T(2,128)(2,1)S(1)}, u32[]{:S(2)}, u32[]{:S(2)}) %all-to-all-start.1) | async-done | bytes 65568 | tf_op jit(solution)/shard_map/all_to_all | solution.py:142
  53.4 3.7 %all-to-all-start.2 = ((bf16[16,2,1024]{2,1,0:T(2,128)(2,1)}), bf16[16,2,1024]{2,1,0:T(2,128)(2,1)S(1)}, u32[]{:S(2)}, u32[]{:S(2)}) async-start(bf16[16,2,1024]{2,1,0:T(2,128)(2,1)} %reshape.280), calls=%async_computation.2 | async-start | bytes 131072 | tf_op jit(solution)/shard_map/all_to_all | solution.py:146
  57.2 7.4 %all-to-all-done.2 = bf16[16,2,1024]{2,1,0:T(2,128)(2,1)S(1)} async-done(((bf16[16,2,1024]{2,1,0:T(2,128)(2,1)}), bf16[16,2,1024]{2,1,0:T(2,128)(2,1)S(1)}, u32[]{:S(2)}, u32[]{:S(2)}) %all-to-all-start.2) | async-done | bytes 65568 | tf_op jit(solution)/shard_map/all_to_all | solution.py:146
  66.0 1.1 reshape.282
  67.1 3.7 %all-to-all-start.3 = ((bf16[16,2,4096]{2,1,0:T(2,128)(2,1)}), bf16[16,2,4096]{2,1,0:T(2,128)(2,1)S(1)}, u32[]{:S(2)}, u32[]{:S(2)}) async-start(bf16[16,2,4096]{2,1,0:T(2,128)(2,1)} %reshape.282), calls=%async_computation.3 | async-start | bytes 524288 | tf_op jit(solution)/shard_map/all_to_all | solution.py:135
  70.8 6.7 %fusion.12 = f32[64,4,64,128]{3,0,2,1:T(8,128)} fusion(bf16[1,4,64,64,128]{4,3,2,1,0:T(8,128)(2,1)} %param.4, bf16[64,64]{1,0:T(8,128)(2,1)S(1)} %copy-done.5), kind=kOutput, calls=%fused_computation.17 | convolution fusion | flops 268435456 | bytes 12591104 | tf_op jit(solution)/shard_map/xycz,co->xyoz/dot_general | solution.py:160
  77.6 4.4 %all-to-all-done.3 = bf16[16,2,4096]{2,1,0:T(2,128)(2,1)S(1)} async-done(((bf16[16,2,4096]{2,1,0:T(2,128)(2,1)}), bf16[16,2,4096]{2,1,0:T(2,128)(2,1)S(1)}, u32[]{:S(2)}, u32[]{:S(2)}) %all-to-all-start.3) | async-done | bytes 262176 | tf_op jit(solution)/shard_map/all_to_all | solution.py:135
  82.3 0.9 fusion.68
  83.6 0.8 add_bitcast_fusion.1
  84.5 2.7 %copy-done.4 = f32[64,4,64,128]{3,0,2,1:T(8,128)S(1)} copy-done((f32[64,4,64,128]{3,0,2,1:T(8,128)S(1)}, f32[64,4,64,128]{3,0,2,1:T(8,128)}, u32[]{:S(2)}) %copy-start.4) | copy-done | bytes 8388632
  87.2 5.5 %fusion.5 = bf16[4,64,64,128]{3,2,1,0:T(8,128)(2,1)S(1)} fusion(f32[64,4,64,128]{3,0,2,1:T(8,128)S(1)} %copy-done.4, bf16[1,4,64,64,128]{4,3,2,1,0:T(8,128)(2,1)S(1)} %copy-done.6, bf16[4,64,64,32]{2,1,3,0:T(8,128)(2,1)S(1)} %add_bitcast_fusion.1, bf16[128,16]{0,1:T(8,128)(2,1)S(1)} %get-tuple-element.20, bf16[128,16]{0,1:T(8,128)(2,1)S(1)} %get-tuple-element.19), kind=kOutput, calls=%fused_computation.7 | convolution fusion | flops 159399936 | bytes 17833984 | tf_op jit(solution)/shard_map/dot_general | solution.py:72
  92.7 4.0 %fusion.101 = f32[4,64,64,32]{2,3,1,0:T(8,128)S(1)} fusion(bf16[4,64,64,128]{3,2,1,0:T(8,128)(2,1)S(1)} %fusion.5, bf16[128,16]{0,1:T(8,128)(2,1)S(1)} %get-tuple-element.21, bf16[128,16]{0,1:T(8,128)(2,1)S(1)} %get-tuple-element.22), kind=kOutput, calls=%fused_computation.141 | convolution fusion | flops 134234112 | bytes 6299648 | tf_op jit(solution)/shard_map/dot_general | solution.py:64
  97.5 0.8 fusion.16
  98.3 2.4 %fusion.41 = bf16[4,16,64,32]{2,1,3,0:T(8,128)(2,1)S(1)} fusion(f32[16,4,64,32]{2,0,3,1:T(8,128)S(1)} %fusion.16, f32[4,64,64,32]{2,3,1,0:T(8,128)S(1)} %fusion.101, s32[16]{0:T(128)S(1)} %compare_select_fusion), kind=kOutput, calls=%fused_computation.45 | convolution fusion | flops 17053696 | bytes 2883648 | tf_op jit(solution)/shard_map/xyck,yj->xjck/dot_general | solution.py:49
  100.8 1.1 reshape.284
  101.9 3.8 %all-to-all-start.4 = ((bf16[16,2,4096]{2,1,0:T(2,128)(2,1)}), bf16[16,2,4096]{2,1,0:T(2,128)(2,1)S(1)}, u32[]{:S(2)}, u32[]{:S(2)}) async-start(bf16[16,2,4096]{2,1,0:T(2,128)(2,1)} %reshape.284), calls=%async_computation.4 | async-start | bytes 524288 | tf_op jit(solution)/shard_map/all_to_all | solution.py:126
  105.8 9.6 %all-to-all-done.4 = bf16[16,2,4096]{2,1,0:T(2,128)(2,1)S(1)} async-done(((bf16[16,2,4096]{2,1,0:T(2,128)(2,1)}), bf16[16,2,4096]{2,1,0:T(2,128)(2,1)S(1)}, u32[]{:S(2)}, u32[]{:S(2)}) %all-to-all-start.4) | async-done | bytes 262176 | tf_op jit(solution)/shard_map/all_to_all | solution.py:126
  117.1 13.4 %all_to_all.109 = bf16[16,2,1024]{2,1,0:T(2,128)(2,1)S(1)} all-to-all(bf16[16,2,1024]{2,1,0:T(2,128)(2,1)S(1)} %reshape.286), channel_id=1, replica_groups=mesh['dp'=16,'pencil'=16] {'dp'}, dimensions={0} | all-to-all | bytes 131072 | tf_op jit(solution)/shard_map/all_to_all | solution.py:142
  131.5 10.2 %all_to_all.110 = bf16[16,2,1024]{2,1,0:T(2,128)(2,1)S(1)} all-to-all(bf16[16,2,1024]{2,1,0:T(2,128)(2,1)S(1)} %reshape.288), channel_id=1, replica_groups=mesh['dp'=16,'pencil'=16] {'dp'}, dimensions={0} | all-to-all | bytes 131072 | tf_op jit(solution)/shard_map/all_to_all | solution.py:146
  143.2 1.1 reshape.290
  144.3 3.5 %all-to-all-start.7 = ((bf16[16,2,4096]{2,1,0:T(2,128)(2,1)}), bf16[16,2,4096]{2,1,0:T(2,128)(2,1)S(1)}, u32[]{:S(2)}, u32[]{:S(2)}) async-start(bf16[16,2,4096]{2,1,0:T(2,128)(2,1)} %reshape.290), calls=%async_computation.7 | async-start | bytes 524288 | tf_op jit(solution)/shard_map/all_to_all | solution.py:135
  148.2 1.1 fusion.40
  149.3 9.8 %all-to-all-done.7 = bf16[16,2,4096]{2,1,0:T(2,128)(2,1)S(1)} async-done(((bf16[16,2,4096]{2,1,0:T(2,128)(2,1)}), bf16[16,2,4096]{2,1,0:T(2,128)(2,1)S(1)}, u32[]{:S(2)}, u32[]{:S(2)}) %all-to-all-start.7) | async-done | bytes 262176 | tf_op jit(solution)/shard_map/all_to_all | solution.py:135
  159.5 0.9 fusion.66
  160.8 0.9 add_bitcast_fusion
  161.7 2.2 %fusion.14 = f32[4,64,64,128]{3,2,1,0:T(8,128)S(1)} fusion(bf16[4,64,64,32]{2,1,3,0:T(8,128)(2,1)S(1)} %add_bitcast_fusion, bf16[128,16]{0,1:T(8,128)(2,1)S(1)} %get-tuple-element.21, bf16[128,16]{0,1:T(8,128)(2,1)S(1)} %get-tuple-element.22), kind=kOutput, calls=%fused_computation.19 | convolution fusion | flops 134234112 | bytes 9445376 | tf_op jit(solution)/shard_map/dot_general | solution.py:72
  163.9 3.2 %fusion.7 = bf16[1,4,64,64,128]{4,3,2,1,0:T(8,128)(2,1)} fusion(f32[4,64,64,128]{3,2,1,0:T(8,128)S(1)} %fusion.14, bf16[4,64,64,128]{3,2,1,0:T(8,128)(2,1)S(1)} %copy-done.2, bf16[64,64]{1,0:T(8,128)(2,1)S(1)} %copy-done.5), kind=kOutput, calls=%fused_computation.11 | convolution fusion | flops 272629760 | bytes 16785408 | tf_op jit(solution)/shard_map/xyoz,co->xycz/dot_general | solution.py:166
  (80 shorter events, 14.5 us)
Async XLA Ops:
  0.6 51.4 %copy-start = (bf16[1,1,16,64,128]{4,3,2,1,0:T(8,128)(2,1)S(1)}, bf16[1,1,16,64,128]{4,3,2,1,0:T(8,128)(2,1)}, u32[]{:S(2)}) copy-start(bf16[1,1,16,64,128]{4,3,2,1,0:T(8,128)(2,1)} %param.6) | copy-start | bytes 786436
  7.5 3.4 %copy-start.3 = (f32[4,64,64,32]{2,1,0,3:T(8,128)S(1)}, f32[4,64,64,32]{2,1,0,3:T(8,128)}, u32[]{:S(2)}) copy-start(f32[4,64,64,32]{2,1,0,3:T(8,128)} %reshape.248) | copy-start | bytes 6291460
  35.4 16.4 %all-to-all-start.1 = ((bf16[16,2,1024]{2,1,0:T(2,128)(2,1)}), bf16[16,2,1024]{2,1,0:T(2,128)(2,1)S(1)}, u32[]{:S(2)}, u32[]{:S(2)}) async-start(bf16[16,2,1024]{2,1,0:T(2,128)(2,1)} %reshape.278), calls=%async_computation.1 | async-start | bytes 131072 | tf_op jit(solution)/shard_map/all_to_all | solution.py:142
  52.0 18.8 %copy-start.5 = (bf16[64,64]{1,0:T(8,128)(2,1)S(1)}, bf16[64,64]{1,0:T(8,128)(2,1)}, u32[]{:S(2)}) copy-start(bf16[64,64]{1,0:T(8,128)(2,1)} %param.7) | copy-start | bytes 24580
  53.4 11.1 %all-to-all-start.2 = ((bf16[16,2,1024]{2,1,0:T(2,128)(2,1)}), bf16[16,2,1024]{2,1,0:T(2,128)(2,1)S(1)}, u32[]{:S(2)}, u32[]{:S(2)}) async-start(bf16[16,2,1024]{2,1,0:T(2,128)(2,1)} %reshape.280), calls=%async_computation.2 | async-start | bytes 131072 | tf_op jit(solution)/shard_map/all_to_all | solution.py:146
  67.1 14.8 %all-to-all-start.3 = ((bf16[16,2,4096]{2,1,0:T(2,128)(2,1)}), bf16[16,2,4096]{2,1,0:T(2,128)(2,1)S(1)}, u32[]{:S(2)}, u32[]{:S(2)}) async-start(bf16[16,2,4096]{2,1,0:T(2,128)(2,1)} %reshape.282), calls=%async_computation.3 | async-start | bytes 524288 | tf_op jit(solution)/shard_map/all_to_all | solution.py:135
  82.3 2.2 %copy-start.6 = (bf16[1,4,64,64,128]{4,3,2,1,0:T(8,128)(2,1)S(1)}, bf16[1,4,64,64,128]{4,3,2,1,0:T(8,128)(2,1)}, u32[]{:S(2)}) copy-start(bf16[1,4,64,64,128]{4,3,2,1,0:T(8,128)(2,1)} %param.5) | copy-start | bytes 12582916
  83.2 4.0 %copy-start.4 = (f32[64,4,64,128]{3,0,2,1:T(8,128)S(1)}, f32[64,4,64,128]{3,0,2,1:T(8,128)}, u32[]{:S(2)}) copy-start(f32[64,4,64,128]{3,0,2,1:T(8,128)} %fusion.12) | copy-start | bytes 25165828
  92.7 4.1 %copy-start.1 = (bf16[4,64,64,128]{3,2,1,0:T(8,128)(2,1)}, bf16[4,64,64,128]{3,2,1,0:T(8,128)(2,1)S(1)}, u32[]{:S(2)}) copy-start(bf16[4,64,64,128]{3,2,1,0:T(8,128)(2,1)S(1)} %fusion.5) | copy-start | bytes 12582916
  101.9 13.4 %all-to-all-start.4 = ((bf16[16,2,4096]{2,1,0:T(2,128)(2,1)}), bf16[16,2,4096]{2,1,0:T(2,128)(2,1)S(1)}, u32[]{:S(2)}, u32[]{:S(2)}) async-start(bf16[16,2,4096]{2,1,0:T(2,128)(2,1)} %reshape.284), calls=%async_computation.4 | async-start | bytes 524288 | tf_op jit(solution)/shard_map/all_to_all | solution.py:126
  144.3 14.8 %all-to-all-start.7 = ((bf16[16,2,4096]{2,1,0:T(2,128)(2,1)}), bf16[16,2,4096]{2,1,0:T(2,128)(2,1)S(1)}, u32[]{:S(2)}, u32[]{:S(2)}) async-start(bf16[16,2,4096]{2,1,0:T(2,128)(2,1)} %reshape.290), calls=%async_computation.7 | async-start | bytes 524288 | tf_op jit(solution)/shard_map/all_to_all | solution.py:135
  161.6 2.2 %copy-start.2 = (bf16[4,64,64,128]{3,2,1,0:T(8,128)(2,1)S(1)}, bf16[4,64,64,128]{3,2,1,0:T(8,128)(2,1)}, u32[]{:S(2)}) copy-start(bf16[4,64,64,128]{3,2,1,0:T(8,128)(2,1)} %copy-done.1) | copy-start | bytes 12582916
where the time goes:
time: 168 us; the launch traced here: 167 us
  blocking collectives  44.1 us (26%)
  matrix products  38.7 us (23%)
  waiting for transfers between devices  38.5 us (23%)
  starting transfers between devices  23.7 us (14%)
  local copies, waits for them, and re-layouts  15.3 us (9%)
  other arithmetic  5.77 us (3%)
    all_to_all x1, blocking collectives, to_modes(): lax.all_to_all(sectioned.astype(jnp.bfloat16), 'pencil', split_axis=1, co...  20.5 us
    all_to_all x2, waiting for transfers between devices, to_grid(): lax.all_to_all(sectioned.astype(jnp.bfloat16), 'pencil', split_axis=0, co...  14.2 us
    all_to_all x1, blocking collectives, to_owner(): lax.all_to_all(coeffs[None], 'dp', split_axis=1, concat_axis=0, tiled=True)  13.4 us
    unnamed x32, local copies, waits for them, and re-layouts  10.8 us
    all_to_all x1, blocking collectives, from_owner(): lax.all_to_all(coeffs.astype(jnp.bfloat16), 'dp', split_axis=0, concat_ax...  10.2 us
    all_to_all x1, waiting for transfers between devices, to_modes(): lax.all_to_all(sectioned.astype(jnp.bfloat16), 'pencil', split_axis=1, co...  9.57 us
    all_to_all x1, starting transfers between devices, to_owner(): lax.all_to_all(coeffs[None], 'dp', split_axis=1, concat_axis=0, tiled=True)  9.02 us
    dot_general x2, matrix products, z_forward(): jnp.dot(field_in.reshape(-1, shape_in[-1]), matrix, preferred_element_typ...  7.76 us
  transfers between devices with their start and end apart: 5, of which 5 were waited for; matrix products, arithmetic and copies ran while one was open for 5% of the time, Pallas kernels for 0%

commit v1 on v0

--- a/solution.py
+++ b/solution.py
@@ -139,7 +139,10 @@
 
 
 def to_owner(coeffs):
-    return lax.all_to_all(coeffs[None], "dp", split_axis=1, concat_axis=0, tiled=True)
+    return jnp.concatenate(
+        lax.all_to_all(jnp.stack(jnp.split(coeffs[None], lax.axis_size("dp"), axis=1)), "dp", 0, 0),
+        axis=0,
+    )
 
 
 def from_owner(coeffs):

time: 168 us -> 169 us (level)
    unnamed x32 -> x62, local copies, waits for them, and re-layouts: 10.8 us -> 11.1 us
where the time goes in v1:
time: 169 us; the launch traced here: 168 us
  blocking collectives  44.1 us (26%)
  matrix products  38.7 us (23%)
  waiting for transfers between devices  38.5 us (23%)
  starting transfers between devices  23.7 us (14%)
  local copies, waits for them, and re-layouts  16 us (9%)
  other arithmetic  5.77 us (3%)
    all_to_all x1, blocking collectives, to_modes(): lax.all_to_all(sectioned.astype(jnp.bfloat16), 'pencil', split_axis=1, co...  20.5 us
    all_to_all x2, waiting for transfers between devices, to_grid(): lax.all_to_all(sectioned.astype(jnp.bfloat16), 'pencil', split_axis=0, co...  14.2 us
    all_to_all x1, blocking collectives, to_owner(): lax.all_to_all(jnp.stack(jnp.split(coeffs[None], lax.axis_size('dp'), axi...  13.3 us
    unnamed x62, local copies, waits for them, and re-layouts  11.1 us
    all_to_all x1, blocking collectives, from_owner(): lax.all_to_all(coeffs.astype(jnp.bfloat16), 'dp', split_axis=0, concat_ax...  10.2 us
    all_to_all x1, waiting for transfers between devices, to_modes(): lax.all_to_all(sectioned.astype(jnp.bfloat16), 'pencil', split_axis=1, co...  9.58 us
    all_to_all x1, starting transfers between devices, to_owner(): lax.all_to_all(jnp.stack(jnp.split(coeffs[None], lax.axis_size('dp'), axi...  9.02 us
    dot_general x2, matrix products, z_forward(): jnp.dot(field_in.reshape(-1, shape_in[-1]), matrix, preferred_element_typ...  7.76 us
  transfers between devices with their start and end apart: 5, of which 5 were waited for; matrix products, arithmetic and copies ran while one was open for 5% of the time, Pallas kernels for 0%

profile of v1, /device:TPU:1, one launch (start us, length us, event | category | flops | bytes accessed | tf_op | source)
XLA Modules:
  0.0 168.1 jit_solution(4288391240555731905)
XLA Ops:
  0.7 3.7 %convolution_bitcast_fusion = f32[16384,32]{0,1:T(8,128)S(1)} fusion(bf16[16384,128]{1,0:T(8,128)(2,1)} %bitcast.306, bf16[128,16]{0,1:T(8,128)(2,1)S(1)} %get-tuple-element.53, bf16[128,16]{0,1:T(8,128)(2,1)S(1)} %get-tuple-element.54), kind=kOutput, calls=%fused_computation | convolution fusion | flops 134234112 | bytes 6299648 | tf_op jit(solution)/shard_map/dot_general | solution.py:64
  4.4 3.0 %reshape.248 = f32[4,64,64,32]{2,1,0,3:T(8,128)} reshape(f32[16384,32]{0,1:T(8,128)S(1)} %convolution_bitcast_fusion) | data formatting | bytes 4194304 | tf_op jit(solution)/shard_map/reshape | solution.py:67
  7.5 3.0 %fusion.229 = (bf16[4,64,64,16]{2,1,3,0:T(8,128)(2,1)S(1)}, bf16[4,64,64,16]{2,1,3,0:T(8,128)(2,1)S(1)}) fusion(f32[4,64,64,32]{2,1,0,3:T(8,128)} %reshape.248), kind=kLoop, calls=%fused_computation.290 | loop fusion | flops 524288 | bytes 4194304 | tf_op jit(solution)/shard_map/slice | solution.py:43
  12.6 20.5 %all_to_all.94 = bf16[16,2,4096]{2,1,0:T(2,128)(2,1)S(1)} all-to-all(bf16[16,2,4096]{2,1,0:T(2,128)(2,1)S(1)} %reshape.278), channel_id=1, replica_groups=mesh['dp'=16,'pencil'=16] {'pencil'}, dimensions={0} | all-to-all | bytes 524288 | tf_op jit(solution)/shard_map/all_to_all | solution.py:126
  35.9 9.0 %all-to-all-start.1 = ((bf16[16,2,1024]{2,1,0:T(2,128)(2,1)}), bf16[16,2,1024]{2,1,0:T(2,128)(2,1)S(1)}, u32[]{:S(2)}, u32[]{:S(2)}) async-start(bf16[16,2,1024]{2,1,0:T(2,128)(2,1)} %reshape.280), calls=%async_computation.1 | async-start | bytes 131072 | tf_op jit(solution)/shard_map/all_to_all | solution.py:143
  44.9 7.4 %all-to-all-done.1 = bf16[16,2,1024]{2,1,0:T(2,128)(2,1)S(1)} async-done(((bf16[16,2,1024]{2,1,0:T(2,128)(2,1)}), bf16[16,2,1024]{2,1,0:T(2,128)(2,1)S(1)}, u32[]{:S(2)}, u32[]{:S(2)}) %all-to-all-start.1) | async-done | bytes 65568 | tf_op jit(solution)/shard_map/all_to_all | solution.py:143
  53.9 3.7 %all-to-all-start.2 = ((bf16[16,2,1024]{2,1,0:T(2,128)(2,1)}), bf16[16,2,1024]{2,1,0:T(2,128)(2,1)S(1)}, u32[]{:S(2)}, u32[]{:S(2)}) async-start(bf16[16,2,1024]{2,1,0:T(2,128)(2,1)} %reshape.282), calls=%async_computation.2 | async-start | bytes 131072 | tf_op jit(solution)/shard_map/all_to_all | solution.py:149
  57.6 7.4 %all-to-all-done.2 = bf16[16,2,1024]{2,1,0:T(2,128)(2,1)S(1)} async-done(((bf16[16,2,1024]{2,1,0:T(2,128)(2,1)}), bf16[16,2,1024]{2,1,0:T(2,128)(2,1)S(1)}, u32[]{:S(2)}, u32[]{:S(2)}) %all-to-all-start.2) | async-done | bytes 65568 | tf_op jit(solution)/shard_map/all_to_all | solution.py:149
  66.5 1.1 reshape.284
  67.6 3.7 %all-to-all-start.3 = ((bf16[16,2,4096]{2,1,0:T(2,128)(2,1)}), bf16[16,2,4096]{2,1,0:T(2,128)(2,1)S(1)}, u32[]{:S(2)}, u32[]{:S(2)}) async-start(bf16[16,2,4096]{2,1,0:T(2,128)(2,1)} %reshape.284), calls=%async_computation.3 | async-start | bytes 524288 | tf_op jit(solution)/shard_map/all_to_all | solution.py:135
  71.3 6.8 %fusion.12 = f32[64,4,64,128]{3,0,2,1:T(8,128)} fusion(bf16[1,4,64,64,128]{4,3,2,1,0:T(8,128)(2,1)} %param.4, bf16[64,64]{1,0:T(8,128)(2,1)S(1)} %copy-done.5), kind=kOutput, calls=%fused_computation.17 | convolution fusion | flops 268435456 | bytes 12591104 | tf_op jit(solution)/shard_map/xycz,co->xyoz/dot_general | solution.py:163
  78.1 4.3 %all-to-all-done.3 = bf16[16,2,4096]{2,1,0:T(2,128)(2,1)S(1)} async-done(((bf16[16,2,4096]{2,1,0:T(2,128)(2,1)}), bf16[16,2,4096]{2,1,0:T(2,128)(2,1)S(1)}, u32[]{:S(2)}, u32[]{:S(2)}) %all-to-all-start.3) | async-done | bytes 262176 | tf_op jit(solution)/shard_map/all_to_all | solution.py:135
  82.8 0.9 fusion.68
  84.1 0.9 add_bitcast_fusion.1
  85.0 2.7 %copy-done.4 = f32[64,4,64,128]{3,0,2,1:T(8,128)S(1)} copy-done((f32[64,4,64,128]{3,0,2,1:T(8,128)S(1)}, f32[64,4,64,128]{3,0,2,1:T(8,128)}, u32[]{:S(2)}) %copy-start.4) | copy-done | bytes 8388632
  87.7 5.5 %fusion.5 = bf16[4,64,64,128]{3,2,1,0:T(8,128)(2,1)S(1)} fusion(f32[64,4,64,128]{3,0,2,1:T(8,128)S(1)} %copy-done.4, bf16[1,4,64,64,128]{4,3,2,1,0:T(8,128)(2,1)S(1)} %copy-done.6, bf16[4,64,64,32]{2,1,3,0:T(8,128)(2,1)S(1)} %add_bitcast_fusion.1, bf16[128,16]{0,1:T(8,128)(2,1)S(1)} %get-tuple-element.52, bf16[128,16]{0,1:T(8,128)(2,1)S(1)} %get-tuple-element.51), kind=kOutput, calls=%fused_computation.7 | convolution fusion | flops 159399936 | bytes 17833984 | tf_op jit(solution)/shard_map/dot_general | solution.py:72
  93.1 4.0 %fusion.101 = f32[4,64,64,32]{2,3,1,0:T(8,128)S(1)} fusion(bf16[4,64,64,128]{3,2,1,0:T(8,128)(2,1)S(1)} %fusion.5, bf16[128,16]{0,1:T(8,128)(2,1)S(1)} %get-tuple-element.53, bf16[128,16]{0,1:T(8,128)(2,1)S(1)} %get-tuple-element.54), kind=kOutput, calls=%fused_computation.173 | convolution fusion | flops 134234112 | bytes 6299648 | tf_op jit(solution)/shard_map/dot_general | solution.py:64
  98.0 0.8 fusion.16
  98.7 2.4 %fusion.41 = bf16[4,16,64,32]{2,1,3,0:T(8,128)(2,1)S(1)} fusion(f32[16,4,64,32]{2,0,3,1:T(8,128)S(1)} %fusion.16, f32[4,64,64,32]{2,3,1,0:T(8,128)S(1)} %fusion.101, s32[16]{0:T(128)S(1)} %compare_select_fusion), kind=kOutput, calls=%fused_computation.45 | convolution fusion | flops 17053696 | bytes 2883648 | tf_op jit(solution)/shard_map/xyck,yj->xjck/dot_general | solution.py:49
  101.3 1.1 reshape.286
  102.4 3.8 %all-to-all-start.4 = ((bf16[16,2,4096]{2,1,0:T(2,128)(2,1)}), bf16[16,2,4096]{2,1,0:T(2,128)(2,1)S(1)}, u32[]{:S(2)}, u32[]{:S(2)}) async-start(bf16[16,2,4096]{2,1,0:T(2,128)(2,1)} %reshape.286), calls=%async_computation.4 | async-start | bytes 524288 | tf_op jit(solution)/shard_map/all_to_all | solution.py:126
  106.2 9.6 %all-to-all-done.4 = bf16[16,2,4096]{2,1,0:T(2,128)(2,1)S(1)} async-done(((bf16[16,2,4096]{2,1,0:T(2,128)(2,1)}), bf16[16,2,4096]{2,1,0:T(2,128)(2,1)S(1)}, u32[]{:S(2)}, u32[]{:S(2)}) %all-to-all-start.4) | async-done | bytes 262176 | tf_op jit(solution)/shard_map/all_to_all | solution.py:126
  118.0 13.3 %all_to_all.95 = bf16[16,2,1024]{2,1,0:T(2,128)(2,1)S(1)} all-to-all(bf16[16,2,1024]{2,1,0:T(2,128)(2,1)S(1)} %reshape.288), channel_id=1, replica_groups=mesh['dp'=16,'pencil'=16] {'dp'}, dimensions={0} | all-to-all | bytes 131072 | tf_op jit(solution)/shard_map/all_to_all | solution.py:143
  132.4 10.2 %all_to_all.96 = bf16[16,2,1024]{2,1,0:T(2,128)(2,1)S(1)} all-to-all(bf16[16,2,1024]{2,1,0:T(2,128)(2,1)S(1)} %reshape.290), channel_id=1, replica_groups=mesh['dp'=16,'pencil'=16] {'dp'}, dimensions={0} | all-to-all | bytes 131072 | tf_op jit(solution)/shard_map/all_to_all | solution.py:149
  144.1 1.1 reshape.292
  145.3 3.5 %all-to-all-start.7 = ((bf16[16,2,4096]{2,1,0:T(2,128)(2,1)}), bf16[16,2,4096]{2,1,0:T(2,128)(2,1)S(1)}, u32[]{:S(2)}, u32[]{:S(2)}) async-start(bf16[16,2,4096]{2,1,0:T(2,128)(2,1)} %reshape.292), calls=%async_computation.7 | async-start | bytes 524288 | tf_op jit(solution)/shard_map/all_to_all | solution.py:135
  149.1 1.1 fusion.40
  150.2 9.8 %all-to-all-done.7 = bf16[16,2,4096]{2,1,0:T(2,128)(2,1)S(1)} async-done(((bf16[16,2,4096]{2,1,0:T(2,128)(2,1)}), bf16[16,2,4096]{2,1,0:T(2,128)(2,1)S(1)}, u32[]{:S(2)}, u32[]{:S(2)}) %all-to-all-start.7) | async-done | bytes 262176 | tf_op jit(solution)/shard_map/all_to_all | solution.py:135
  160.4 0.9 fusion.66
  161.7 0.9 add_bitcast_fusion
  162.6 2.2 %fusion.14 = f32[4,64,64,128]{3,2,1,0:T(8,128)S(1)} fusion(bf16[4,64,64,32]{2,1,3,0:T(8,128)(2,1)S(1)} %add_bitcast_fusion, bf16[128,16]{0,1:T(8,128)(2,1)S(1)} %get-tuple-element.53, bf16[128,16]{0,1:T(8,128)(2,1)S(1)} %get-tuple-element.54), kind=kOutput, calls=%fused_computation.19 | convolution fusion | flops 134234112 | bytes 9445376 | tf_op jit(solution)/shard_map/dot_general | solution.py:72
  164.8 3.3 %fusion.7 = bf16[1,4,64,64,128]{4,3,2,1,0:T(8,128)(2,1)} fusion(f32[4,64,64,128]{3,2,1,0:T(8,128)S(1)} %fusion.14, bf16[4,64,64,128]{3,2,1,0:T(8,128)(2,1)S(1)} %copy-done.2, bf16[64,64]{1,0:T(8,128)(2,1)S(1)} %copy-done.5), kind=kOutput, calls=%fused_computation.11 | convolution fusion | flops 272629760 | bytes 16785408 | tf_op jit(solution)/shard_map/xyoz,co->xycz/dot_general | solution.py:169
  (112 shorter events, 15.3 us)
Async XLA Ops:
  0.6 51.8 %copy-start = (bf16[1,1,16,64,128]{4,3,2,1,0:T(8,128)(2,1)S(1)}, bf16[1,1,16,64,128]{4,3,2,1,0:T(8,128)(2,1)}, u32[]{:S(2)}) copy-start(bf16[1,1,16,64,128]{4,3,2,1,0:T(8,128)(2,1)} %param.6) | copy-start | bytes 786436
  7.5 3.4 %copy-start.3 = (f32[4,64,64,32]{2,1,0,3:T(8,128)S(1)}, f32[4,64,64,32]{2,1,0,3:T(8,128)}, u32[]{:S(2)}) copy-start(f32[4,64,64,32]{2,1,0,3:T(8,128)} %reshape.248) | copy-start | bytes 6291460
  35.9 16.4 %all-to-all-start.1 = ((bf16[16,2,1024]{2,1,0:T(2,128)(2,1)}), bf16[16,2,1024]{2,1,0:T(2,128)(2,1)S(1)}, u32[]{:S(2)}, u32[]{:S(2)}) async-start(bf16[16,2,1024]{2,1,0:T(2,128)(2,1)} %reshape.280), calls=%async_computation.1 | async-start | bytes 131072 | tf_op jit(solution)/shard_map/all_to_all | solution.py:143
  52.5 18.8 %copy-start.5 = (bf16[64,64]{1,0:T(8,128)(2,1)S(1)}, bf16[64,64]{1,0:T(8,128)(2,1)}, u32[]{:S(2)}) copy-start(bf16[64,64]{1,0:T(8,128)(2,1)} %param.7) | copy-start | bytes 24580
  53.9 11.1 %all-to-all-start.2 = ((bf16[16,2,1024]{2,1,0:T(2,128)(2,1)}), bf16[16,2,1024]{2,1,0:T(2,128)(2,1)S(1)}, u32[]{:S(2)}, u32[]{:S(2)}) async-start(bf16[16,2,1024]{2,1,0:T(2,128)(2,1)} %reshape.282), calls=%async_computation.2 | async-start | bytes 131072 | tf_op jit(solution)/shard_map/all_to_all | solution.py:149
  67.6 14.8 %all-to-all-start.3 = ((bf16[16,2,4096]{2,1,0:T(2,128)(2,1)}), bf16[16,2,4096]{2,1,0:T(2,128)(2,1)S(1)}, u32[]{:S(2)}, u32[]{:S(2)}) async-start(bf16[16,2,4096]{2,1,0:T(2,128)(2,1)} %reshape.284), calls=%async_computation.3 | async-start | bytes 524288 | tf_op jit(solution)/shard_map/all_to_all | solution.py:135
  82.8 2.2 %copy-start.6 = (bf16[1,4,64,64,128]{4,3,2,1,0:T(8,128)(2,1)S(1)}, bf16[1,4,64,64,128]{4,3,2,1,0:T(8,128)(2,1)}, u32[]{:S(2)}) copy-start(bf16[1,4,64,64,128]{4,3,2,1,0:T(8,128)(2,1)} %param.5) | copy-start | bytes 12582916
  83.7 4.0 %copy-start.4 = (f32[64,4,64,128]{3,0,2,1:T(8,128)S(1)}, f32[64,4,64,128]{3,0,2,1:T(8,128)}, u32[]{:S(2)}) copy-start(f32[64,4,64,128]{3,0,2,1:T(8,128)} %fusion.12) | copy-start | bytes 25165828
  93.1 4.1 %copy-start.1 = (bf16[4,64,64,128]{3,2,1,0:T(8,128)(2,1)}, bf16[4,64,64,128]{3,2,1,0:T(8,128)(2,1)S(1)}, u32[]{:S(2)}) copy-start(bf16[4,64,64,128]{3,2,1,0:T(8,128)(2,1)S(1)} %fusion.5) | copy-start | bytes 12582916
  102.4 13.4 %all-to-all-start.4 = ((bf16[16,2,4096]{2,1,0:T(2,128)(2,1)}), bf16[16,2,4096]{2,1,0:T(2,128)(2,1)S(1)}, u32[]{:S(2)}, u32[]{:S(2)}) async-start(bf16[16,2,4096]{2,1,0:T(2,128)(2,1)} %reshape.286), calls=%async_computation.4 | async-start | bytes 524288 | tf_op jit(solution)/shard_map/all_to_all | solution.py:126
  145.3 14.8 %all-to-all-start.7 = ((bf16[16,2,4096]{2,1,0:T(2,128)(2,1)}), bf16[16,2,4096]{2,1,0:T(2,128)(2,1)S(1)}, u32[]{:S(2)}, u32[]{:S(2)}) async-start(bf16[16,2,4096]{2,1,0:T(2,128)(2,1)} %reshape.292), calls=%async_computation.7 | async-start | bytes 524288 | tf_op jit(solution)/shard_map/all_to_all | solution.py:135
  162.6 2.2 %copy-start.2 = (bf16[4,64,64,128]{3,2,1,0:T(8,128)(2,1)S(1)}, bf16[4,64,64,128]{3,2,1,0:T(8,128)(2,1)}, u32[]{:S(2)}) copy-start(bf16[4,64,64,128]{3,2,1,0:T(8,128)(2,1)} %copy-done.1) | copy-start | bytes 12582916
